TPU v7x, 256 devices: a whole 4x4x8 slice. The times are simulated.
256 devices in a mesh: blk: 128 (over y, x_hi, z, core), row: 2 (over x_lo).
Axes of the slice: x: 4 (x_hi: 2, x_lo: 2; x = x_hi * 2 + x_lo), y: 4, z: 8, core: 2. Of those that a mesh axis runs over, the one named last changes fastest.
Arguments:
- features: bfloat16 [12288, 16384], P('row', 'blk'), parts along dimension 0, may hold values from -6 to 6
- link_values: bfloat16 [8, 32, 16384], P(None, None, 'blk'), may hold values from -1 to 1
- link_columns: int32 [8, 32, 16384], P(None, None, 'blk'), may hold values from 0 to 255
- layer_bias: float32 [8, 16384], P(None, 'blk'), may hold values from -0.5 to 0.5
Outputs:
- outputs: bfloat16 [12288, 16384], P('row', 'blk'), parts along dimension 0
There are 2 independent parts, one for each index of `row`. A program takes and returns all parts, laid end to end along the dimension named above; an argument that names none is the same for every part. Nothing has to cross between parts.
All inputs are finite; a program needn't handle non-finite values.
Results may differ from a plain program's by a relative error of at most 0.0072.
Values may be sent and summed in bfloat16 or wider, within the bound.
A program may use at most 64 MiB of HBM per device.

v0:
```python
import jax
import jax.numpy as jnp
from jax import lax
from jax.sharding import PartitionSpec as P

LAYERS = 8


ceiling_value = 4.0


def partner_2(value, axis, bit):
    mask = 2**bit
    pairs = [(source, source ^ mask) for source in range(lax.axis_size(axis))]
    return lax.ppermute(value, axis, pairs)


def dense_block(values_layer, columns_layer):
    block_width = values_layer.shape[1]
    columns = lax.broadcasted_iota(jnp.int32, (1, 2 * block_width, 1), 1)
    onehot = columns_layer[:, None, :] == columns
    summed = jnp.sum(jnp.where(onehot, values_layer.astype(jnp.float32)[:, None, :], 0.0), axis=0)
    return summed.astype(jnp.bfloat16)


def finish(own_part, peer_part, bias_row):
    preact = own_part + peer_part + bias_row[None, :]
    return jnp.minimum(jnp.maximum(preact, 0.0), ceiling_value).astype(jnp.bfloat16)


def shards(features, link_values, link_columns, layer_bias):
    block_width = features.shape[1]
    block_count = lax.axis_size("blk")
    bit_count = block_count.bit_length() - 1
    blocks = features
    for layer_at in range(LAYERS):
        bit_at = layer_at % bit_count
        weights = dense_block(link_values[layer_at], link_columns[layer_at])
        bias_row = layer_bias[layer_at]
        half_count = blocks.shape[0] // 2
        pieces = []
        for part_at in range(2):
            half_rows = blocks[part_at * half_count : (part_at + 1) * half_count]
            partner = partner_2(half_rows, "blk", bit_at)
            own_part = jnp.dot(half_rows, weights[:block_width], preferred_element_type=jnp.float32)
            peer_part = jnp.dot(partner, weights[block_width:], preferred_element_type=jnp.float32)
            pieces.append(finish(own_part, peer_part, bias_row))
        blocks = jnp.concatenate(pieces, axis=0)
    return blocks


def solution(mesh):
    return jax.shard_map(
        shards,
        mesh=mesh,
        in_specs=(P("row", "blk"), P(None, None, "blk"), P(None, None, "blk"), P(None, "blk")),
        out_specs=P("row", "blk"),
        check_vma=False,
    )
```

profile of v0, /device:TPU:97, one launch (start us, length us, event | category | flops | bytes accessed | tf_op | source)
XLA Modules:
  0.0 297.2 jit_solution(7785523257444493915)
XLA Ops:
  0.0 1.6 fusion.98
  1.6 0.8 collective-permute-start
  2.6 0.5 select_reduce_fusion.7
  3.1 0.5 select_reduce_fusion.6
  3.6 0.5 select_reduce_fusion.5
  4.2 0.5 select_reduce_fusion.4
  4.7 0.5 select_reduce_fusion.3
  5.3 0.5 select_reduce_fusion.2
  6.8 0.5 select_reduce_fusion
  8.6 1.5 collective-permute-start.9
  11.0 15.9 %collective-permute-done.1 = bf16[3072,128]{0,1:T(8,128)(2,1)S(1)} collective-permute-done((bf16[3072,128]{0,1:T(8,128)(2,1)S(1)}, bf16[3072,128]{0,1:T(8,128)(2,1)S(1)}, u32[]{:S(2)}, u32[]{:S(2)}) %collective-permute-start.1) | collective-permute-done | bytes 786464 | tf_op jit(solution)/shard_map/ppermute | solution.py:15
  27.4 29.1 %collective-permute-done.9 = bf16[3072,128]{0,1:T(8,128)(2,1)S(1)} collective-permute-done((bf16[3072,128]{0,1:T(8,128)(2,1)S(1)}, bf16[3072,128]{0,1:T(8,128)(2,1)S(1)}, u32[]{:S(2)}, u32[]{:S(2)}) %collective-permute-start.9) | collective-permute-done | bytes 786464 | tf_op jit(solution)/shard_map/ppermute | solution.py:15
  57.0 0.8 collective-permute-start.10
  58.5 88.0 %collective-permute-done.2 = bf16[3072,128]{1,0:T(8,128)(2,1)S(1)} collective-permute-done((bf16[3072,128]{1,0:T(8,128)(2,1)S(1)}, bf16[3072,128]{1,0:T(8,128)(2,1)S(1)}, u32[]{:S(2)}, u32[]{:S(2)}) %collective-permute-start.2) | collective-permute-done | bytes 786464 | tf_op jit(solution)/shard_map/ppermute | solution.py:15
  147.2 16.2 %collective-permute-done.10 = bf16[3072,128]{1,0:T(8,128)(2,1)S(1)} collective-permute-done((bf16[3072,128]{1,0:T(8,128)(2,1)S(1)}, bf16[3072,128]{1,0:T(8,128)(2,1)S(1)}, u32[]{:S(2)}, u32[]{:S(2)}) %collective-permute-start.10) | collective-permute-done | bytes 786464 | tf_op jit(solution)/shard_map/ppermute | solution.py:15
  163.7 4.3 %collective-permute-start.11 = (bf16[3072,128]{1,0:T(8,128)(2,1)S(1)}, bf16[3072,128]{1,0:T(8,128)(2,1)S(1)}, u32[]{:S(2)}, u32[]{:S(2)}) collective-permute-start(bf16[3072,128]{1,0:T(8,128)(2,1)S(1)} %fusion.42), channel_id=1, source_target_pairs={{0,16},{2,18},{4,20},{6,22},{8,24},{10,26},{12,28},{14,30},{16,0},... | collective-permute-start | bytes 2359304 | tf_op jit(solution)/shard_map/ppermute | solution.py:15
  168.8 17.9 %collective-permute-done.3 = bf16[3072,128]{1,0:T(8,128)(2,1)S(1)} collective-permute-done((bf16[3072,128]{1,0:T(8,128)(2,1)S(1)}, bf16[3072,128]{1,0:T(8,128)(2,1)S(1)}, u32[]{:S(2)}, u32[]{:S(2)}) %collective-permute-start.3) | collective-permute-done | bytes 786464 | tf_op jit(solution)/shard_map/ppermute | solution.py:15
  187.1 2.8 collective-permute-start.4
  189.8 25.8 %collective-permute-done.11 = bf16[3072,128]{1,0:T(8,128)(2,1)S(1)} collective-permute-done((bf16[3072,128]{1,0:T(8,128)(2,1)S(1)}, bf16[3072,128]{1,0:T(8,128)(2,1)S(1)}, u32[]{:S(2)}, u32[]{:S(2)}) %collective-permute-start.11) | collective-permute-done | bytes 786464 | tf_op jit(solution)/shard_map/ppermute | solution.py:15
  216.1 3.0 %collective-permute-start.12 = (bf16[3072,128]{1,0:T(8,128)(2,1)S(1)}, bf16[3072,128]{1,0:T(8,128)(2,1)S(1)}, u32[]{:S(2)}, u32[]{:S(2)}) collective-permute-start(bf16[3072,128]{1,0:T(8,128)(2,1)S(1)} %fusion.43), channel_id=1, source_target_pairs={{0,32},{2,34},{4,36},{6,38},{8,40},{10,42},{12,44},{14,46},{16,48}... | collective-permute-start | bytes 2359304 | tf_op jit(solution)/shard_map/ppermute | solution.py:15
  220.1 1.3 collective-permute-start.5
  221.5 11.8 %collective-permute-done.12 = bf16[3072,128]{1,0:T(8,128)(2,1)S(1)} collective-permute-done((bf16[3072,128]{1,0:T(8,128)(2,1)S(1)}, bf16[3072,128]{1,0:T(8,128)(2,1)S(1)}, u32[]{:S(2)}, u32[]{:S(2)}) %collective-permute-start.12) | collective-permute-done | bytes 786464 | tf_op jit(solution)/shard_map/ppermute | solution.py:15
  233.6 1.5 collective-permute-start.13
  236.2 2.8 collective-permute-start.6
  239.0 14.3 %collective-permute-done.13 = bf16[3072,128]{1,0:T(8,128)(2,1)S(1)} collective-permute-done((bf16[3072,128]{1,0:T(8,128)(2,1)S(1)}, bf16[3072,128]{1,0:T(8,128)(2,1)S(1)}, u32[]{:S(2)}, u32[]{:S(2)}) %collective-permute-start.13) | collective-permute-done | bytes 786464 | tf_op jit(solution)/shard_map/ppermute | solution.py:15
  253.7 3.0 %collective-permute-start.14 = (bf16[3072,128]{1,0:T(8,128)(2,1)S(1)}, bf16[3072,128]{1,0:T(8,128)(2,1)S(1)}, u32[]{:S(2)}, u32[]{:S(2)}) collective-permute-start(bf16[3072,128]{1,0:T(8,128)(2,1)S(1)} %fusion.45), channel_id=1, source_target_pairs={{0,128},{2,130},{4,132},{6,134},{8,136},{10,138},{12,140},{14,142}... | collective-permute-start | bytes 2359304 | tf_op jit(solution)/shard_map/ppermute | solution.py:15
  257.4 15.2 %collective-permute-done.6 = bf16[3072,128]{1,0:T(8,128)(2,1)S(1)} collective-permute-done((bf16[3072,128]{1,0:T(8,128)(2,1)S(1)}, bf16[3072,128]{1,0:T(8,128)(2,1)S(1)}, u32[]{:S(2)}, u32[]{:S(2)}) %collective-permute-start.6) | collective-permute-done | bytes 786464 | tf_op jit(solution)/shard_map/ppermute | solution.py:15
  273.0 7.1 %collective-permute-start.7 = (bf16[3072,128]{1,0:T(8,128)(2,1)S(1)}, bf16[3072,128]{1,0:T(8,128)(2,1)S(1)}, u32[]{:S(2)}, u32[]{:S(2)}) collective-permute-start(bf16[3072,128]{1,0:T(8,128)(2,1)S(1)} %fusion.38), channel_id=1, source_target_pairs={{0,2},{2,0},{4,6},{6,4},{8,10},{10,8},{12,14},{14,12},{16,18},{18,... | collective-permute-start | bytes 2359304 | tf_op jit(solution)/shard_map/ppermute | solution.py:15
  280.1 9.4 %collective-permute-done.14 = bf16[3072,128]{1,0:T(8,128)(2,1)S(1)} collective-permute-done((bf16[3072,128]{1,0:T(8,128)(2,1)S(1)}, bf16[3072,128]{1,0:T(8,128)(2,1)S(1)}, u32[]{:S(2)}, u32[]{:S(2)}) %collective-permute-start.14) | collective-permute-done | bytes 786464 | tf_op jit(solution)/shard_map/ppermute | solution.py:15
  289.8 3.8 %collective-permute-start.15 = (bf16[3072,128]{1,0:T(8,128)(2,1)S(1)}, bf16[3072,128]{1,0:T(8,128)(2,1)S(1)}, u32[]{:S(2)}, u32[]{:S(2)}) collective-permute-start(bf16[3072,128]{1,0:T(8,128)(2,1)S(1)} %fusion.46), channel_id=1, source_target_pairs={{0,2},{2,0},{4,6},{6,4},{8,10},{10,8},{12,14},{14,12},{16,18},{18,... | collective-permute-start | bytes 2359304 | tf_op jit(solution)/shard_map/ppermute | solution.py:15
  294.7 0.8 collective-permute-done.15
  295.9 1.2 pad_maximum_fusion
  (53 shorter events, 13.0 us)
Async XLA Ops:
  0.0 6.4 %copy-start = (bf16[6144,128]{1,0:T(8,128)(2,1)S(1)}, bf16[6144,128]{1,0:T(8,128)(2,1)}, u32[]{:S(2)}) copy-start(bf16[6144,128]{1,0:T(8,128)(2,1)} %param.4) | copy-start | bytes 4718596
  0.0 2.5 copy-start.1
  0.0 2.5 copy-start.2
  0.0 2.5 copy-start.3
  1.6 6.1 %collective-permute-start = (bf16[3072,128]{1,0:T(8,128)(2,1)S(1)}, bf16[3072,128]{1,0:T(8,128)(2,1)S(1)}, u32[]{:S(2)}, u32[]{:S(2)}) collective-permute-start(bf16[3072,128]{1,0:T(8,128)(2,1)S(1)} %get-tuple-element.5), channel_id=1, source_target_pairs={{0,2},{2,0},{4,6},{6,4},{8,10},{10,8},{12,14},{14,12},{16,18},{18,... | collective-permute-start | bytes 2359304 | tf_op jit(solution)/shard_map/ppermute | solution.py:15
  2.4 5.8 %collective-permute-start.8 = (bf16[3072,128]{1,0:T(8,128)(2,1)S(1)}, bf16[3072,128]{1,0:T(8,128)(2,1)S(1)}, u32[]{:S(2)}, u32[]{:S(2)}) collective-permute-start(bf16[3072,128]{1,0:T(8,128)(2,1)S(1)} %get-tuple-element.6), channel_id=1, source_target_pairs={{0,2},{2,0},{4,6},{6,4},{8,10},{10,8},{12,14},{14,12},{16,18},{18,... | collective-permute-start | bytes 2359304 | tf_op jit(solution)/shard_map/ppermute | solution.py:15
  8.1 18.8 %collective-permute-start.1 = (bf16[3072,128]{0,1:T(8,128)(2,1)S(1)}, bf16[3072,128]{0,1:T(8,128)(2,1)S(1)}, u32[]{:S(2)}, u32[]{:S(2)}) collective-permute-start(bf16[3072,128]{0,1:T(8,128)(2,1)S(1)} %bitcast.88), channel_id=1, source_target_pairs={{0,4},{2,6},{4,0},{6,2},{8,12},{10,14},{12,8},{14,10},{16,20},{18,... | collective-permute-start | bytes 2359304 | tf_op jit(solution)/shard_map/ppermute | solution.py:15
  8.6 47.9 %collective-permute-start.9 = (bf16[3072,128]{0,1:T(8,128)(2,1)S(1)}, bf16[3072,128]{0,1:T(8,128)(2,1)S(1)}, u32[]{:S(2)}, u32[]{:S(2)}) collective-permute-start(bf16[3072,128]{0,1:T(8,128)(2,1)S(1)} %bitcast.89), channel_id=1, source_target_pairs={{0,4},{2,6},{4,0},{6,2},{8,12},{10,14},{12,8},{14,10},{16,20},{18,... | collective-permute-start | bytes 2359304 | tf_op jit(solution)/shard_map/ppermute | solution.py:15
  27.3 119.2 %collective-permute-start.2 = (bf16[3072,128]{1,0:T(8,128)(2,1)S(1)}, bf16[3072,128]{1,0:T(8,128)(2,1)S(1)}, u32[]{:S(2)}, u32[]{:S(2)}) collective-permute-start(bf16[3072,128]{1,0:T(8,128)(2,1)S(1)} %fusion.33), channel_id=1, source_target_pairs={{0,8},{2,10},{4,12},{6,14},{8,0},{10,2},{12,4},{14,6},{16,24},{18,... | collective-permute-start | bytes 2359304 | tf_op jit(solution)/shard_map/ppermute | solution.py:15
  57.0 106.4 %collective-permute-start.10 = (bf16[3072,128]{1,0:T(8,128)(2,1)S(1)}, bf16[3072,128]{1,0:T(8,128)(2,1)S(1)}, u32[]{:S(2)}, u32[]{:S(2)}) collective-permute-start(bf16[3072,128]{1,0:T(8,128)(2,1)S(1)} %fusion.41), channel_id=1, source_target_pairs={{0,8},{2,10},{4,12},{6,14},{8,0},{10,2},{12,4},{14,6},{16,24},{18,... | collective-permute-start | bytes 2359304 | tf_op jit(solution)/shard_map/ppermute | solution.py:15
  146.9 39.8 %collective-permute-start.3 = (bf16[3072,128]{1,0:T(8,128)(2,1)S(1)}, bf16[3072,128]{1,0:T(8,128)(2,1)S(1)}, u32[]{:S(2)}, u32[]{:S(2)}) collective-permute-start(bf16[3072,128]{1,0:T(8,128)(2,1)S(1)} %fusion.34), channel_id=1, source_target_pairs={{0,16},{2,18},{4,20},{6,22},{8,24},{10,26},{12,28},{14,30},{16,0},... | collective-permute-start | bytes 2359304 | tf_op jit(solution)/shard_map/ppermute | solution.py:15
  163.7 51.9 %collective-permute-start.11 = (bf16[3072,128]{1,0:T(8,128)(2,1)S(1)}, bf16[3072,128]{1,0:T(8,128)(2,1)S(1)}, u32[]{:S(2)}, u32[]{:S(2)}) collective-permute-start(bf16[3072,128]{1,0:T(8,128)(2,1)S(1)} %fusion.42), channel_id=1, source_target_pairs={{0,16},{2,18},{4,20},{6,22},{8,24},{10,26},{12,28},{14,30},{16,0},... | collective-permute-start | bytes 2359304 | tf_op jit(solution)/shard_map/ppermute | solution.py:15
  187.1 32.7 %collective-permute-start.4 = (bf16[3072,128]{1,0:T(8,128)(2,1)S(1)}, bf16[3072,128]{1,0:T(8,128)(2,1)S(1)}, u32[]{:S(2)}, u32[]{:S(2)}) collective-permute-start(bf16[3072,128]{1,0:T(8,128)(2,1)S(1)} %fusion.35), channel_id=1, source_target_pairs={{0,32},{2,34},{4,36},{6,38},{8,40},{10,42},{12,44},{14,46},{16,48}... | collective-permute-start | bytes 2359304 | tf_op jit(solution)/shard_map/ppermute | solution.py:15
  216.1 17.2 %collective-permute-start.12 = (bf16[3072,128]{1,0:T(8,128)(2,1)S(1)}, bf16[3072,128]{1,0:T(8,128)(2,1)S(1)}, u32[]{:S(2)}, u32[]{:S(2)}) collective-permute-start(bf16[3072,128]{1,0:T(8,128)(2,1)S(1)} %fusion.43), channel_id=1, source_target_pairs={{0,32},{2,34},{4,36},{6,38},{8,40},{10,42},{12,44},{14,46},{16,48}... | collective-permute-start | bytes 2359304 | tf_op jit(solution)/shard_map/ppermute | solution.py:15
  220.1 15.7 %collective-permute-start.5 = (bf16[3072,128]{1,0:T(8,128)(2,1)S(1)}, bf16[3072,128]{1,0:T(8,128)(2,1)S(1)}, u32[]{:S(2)}, u32[]{:S(2)}) collective-permute-start(bf16[3072,128]{1,0:T(8,128)(2,1)S(1)} %fusion.36), channel_id=1, source_target_pairs={{0,64},{2,66},{4,68},{6,70},{8,72},{10,74},{12,76},{14,78},{16,80}... | collective-permute-start | bytes 2359304 | tf_op jit(solution)/shard_map/ppermute | solution.py:15
  233.6 19.6 %collective-permute-start.13 = (bf16[3072,128]{1,0:T(8,128)(2,1)S(1)}, bf16[3072,128]{1,0:T(8,128)(2,1)S(1)}, u32[]{:S(2)}, u32[]{:S(2)}) collective-permute-start(bf16[3072,128]{1,0:T(8,128)(2,1)S(1)} %fusion.44), channel_id=1, source_target_pairs={{0,64},{2,66},{4,68},{6,70},{8,72},{10,74},{12,76},{14,78},{16,80}... | collective-permute-start | bytes 2359304 | tf_op jit(solution)/shard_map/ppermute | solution.py:15
  236.2 36.4 %collective-permute-start.6 = (bf16[3072,128]{1,0:T(8,128)(2,1)S(1)}, bf16[3072,128]{1,0:T(8,128)(2,1)S(1)}, u32[]{:S(2)}, u32[]{:S(2)}) collective-permute-start(bf16[3072,128]{1,0:T(8,128)(2,1)S(1)} %fusion.37), channel_id=1, source_target_pairs={{0,128},{2,130},{4,132},{6,134},{8,136},{10,138},{12,140},{14,142}... | collective-permute-start | bytes 2359304 | tf_op jit(solution)/shard_map/ppermute | solution.py:15
  253.7 35.8 %collective-permute-start.14 = (bf16[3072,128]{1,0:T(8,128)(2,1)S(1)}, bf16[3072,128]{1,0:T(8,128)(2,1)S(1)}, u32[]{:S(2)}, u32[]{:S(2)}) collective-permute-start(bf16[3072,128]{1,0:T(8,128)(2,1)S(1)} %fusion.45), channel_id=1, source_target_pairs={{0,128},{2,130},{4,132},{6,134},{8,136},{10,138},{12,140},{14,142}... | collective-permute-start | bytes 2359304 | tf_op jit(solution)/shard_map/ppermute | solution.py:15
  273.0 21.4 %collective-permute-start.7 = (bf16[3072,128]{1,0:T(8,128)(2,1)S(1)}, bf16[3072,128]{1,0:T(8,128)(2,1)S(1)}, u32[]{:S(2)}, u32[]{:S(2)}) collective-permute-start(bf16[3072,128]{1,0:T(8,128)(2,1)S(1)} %fusion.38), channel_id=1, source_target_pairs={{0,2},{2,0},{4,6},{6,4},{8,10},{10,8},{12,14},{14,12},{16,18},{18,... | collective-permute-start | bytes 2359304 | tf_op jit(solution)/shard_map/ppermute | solution.py:15
  289.8 5.7 %collective-permute-start.15 = (bf16[3072,128]{1,0:T(8,128)(2,1)S(1)}, bf16[3072,128]{1,0:T(8,128)(2,1)S(1)}, u32[]{:S(2)}, u32[]{:S(2)}) collective-permute-start(bf16[3072,128]{1,0:T(8,128)(2,1)S(1)} %fusion.46), channel_id=1, source_target_pairs={{0,2},{2,0},{4,6},{6,4},{8,10},{10,8},{12,14},{14,12},{16,18},{18,... | collective-permute-start | bytes 2359304 | tf_op jit(solution)/shard_map/ppermute | solution.py:15
where the time goes:
time: 297 us
  waiting for transfers between devices  245 us (82%)
  starting transfers between devices  33.3 us (11%)
  matrix products  11.9 us (4%)
  other arithmetic  5.6 us (2%)
    ppermute x16, waiting for transfers between devices, partner_2(): return lax.ppermute(value, axis, pairs)  245 us
    ppermute x16, starting transfers between devices, partner_2(): return lax.ppermute(value, axis, pairs)  33.3 us
    dot_general x16, matrix products, shards(): jnp.dot(partner, weights[block_width:], preferred_element_type=jnp.float32)  6.11 us
  transfers between devices with their start and end apart: 16, of which 11 were waited for; matrix products, arithmetic and copies ran while one was open for 5% of the time, Pallas kernels for 0%

commit v1 on v0

v1 whole, which is shorter than its diff:
```python
import functools

import jax
import jax.numpy as jnp
from jax import lax
from jax.experimental import pallas as pl
from jax.experimental.pallas import tpu as pltpu
from jax.sharding import PartitionSpec as P

MESH = pl.DeviceIdType.MESH
LAYERS = 8
CEILING = 4.0
CHUNKS = 8
GROUP = 8
MASKS = (1, 2, 4)


def bits(value):
    return [(value // 2**k) % 2 for k in range(3)]


def xor(value_bits, mask):
    total = 0
    for k in range(3):
        flip = (mask >> k) & 1 if isinstance(mask, int) else mask[k]
        total = total + ((value_bits[k] + flip) % 2) * 2**k
    return total


def dense(values, columns):
    fan_in, width = values.shape
    field = lax.broadcasted_iota(jnp.int32, (2 * width, width), 0).astype(jnp.float32)
    total = jnp.zeros((2 * width, width), jnp.float32)
    for link in range(fan_in):
        total = total + jnp.where(field == columns[link : link + 1, :], values[link : link + 1, :], 0.0)
    return total.astype(jnp.bfloat16)


def activate(preact):
    return jnp.minimum(jnp.maximum(preact, 0.0), CEILING).astype(jnp.bfloat16)


def three_layers(slots, weights, bias, first_layer):
    width = slots[0].shape[1]
    for step, mask in enumerate(MASKS):
        after = [None] * GROUP
        for low in range(GROUP):
            if low & mask:
                continue
            high = low | mask
            w_low, w_high = weights[low, step], weights[high, step]
            w_high = jnp.concatenate([w_high[width:], w_high[:width]], axis=0)
            row = first_layer + step
            b_pair = jnp.concatenate([bias[low, row : row + 1, :], bias[high, row : row + 1, :]], axis=1)
            pair = jnp.dot(
                jnp.concatenate([slots[low], slots[high]], axis=1),
                jnp.concatenate([w_low, w_high], axis=1),
                preferred_element_type=jnp.float32,
            )
            pair = activate(pair + b_pair)
            after[low], after[high] = pair[:, :width], pair[:, width:]
        slots = after
    return slots


def kernel(
    features, values, columns, bias, out,
    partner_in, act0, z_in, z_out, back, x_in, x_out, home, partner_home,
    own_columns, z_values, z_columns, z_bias, x_bias, w_end, w_z, w_x,
    pf_s, pf_r, zi_s, zi_r, zo_s, zo_r, xi_s, xi_r, xo_s, xo_r, pl_s, pl_r, w_s, w_r,
):
    chunks, _, piece, width = features.shape
    block = lax.axis_index("blk")
    core, z, u = block % 2, (block // 2) % GROUP, block // (2 * GROUP)
    zb, ub = bits(z), bits(u)
    partner = block + 1 - 2 * core
    z_of = [xor(zb, j) for j in range(GROUP)]
    u_of = [xor(ub, j) for j in range(GROUP)]
    z_peer = [(u * GROUP + z_of[j]) * 2 + core for j in range(GROUP)]
    u_peer = [(u_of[j] * GROUP + z) * 2 + core for j in range(GROUP)]

    def copy(src, dst, send, recv, peer):
        return pltpu.make_async_remote_copy(
            src_ref=src, dst_ref=dst, send_sem=send, recv_sem=recv, device_id={"blk": peer}, device_id_type=MESH
        )

    barrier = pltpu.get_barrier_semaphore()
    peers = [partner, *z_peer[1:], *u_peer[1:]]
    for peer in peers:
        pl.semaphore_signal(barrier, inc=1, device_id={"blk": peer}, device_id_type=MESH)
    own_columns[...] = columns[...].astype(jnp.float32).astype(jnp.bfloat16)
    z_values[0] = values[1:4]
    z_columns[0] = columns[1:4].astype(jnp.float32).astype(jnp.bfloat16)
    z_bias[0] = bias[...]
    x_bias[0] = bias[...]
    pl.semaphore_wait(barrier, len(peers))

    def partner_copy(c):
        return copy(features.at[c], partner_in.at[c], pf_s.at[c], pf_r.at[c], partner)

    partner_copy(0).start()
    for j in range(1, GROUP):
        copy(bias, z_bias.at[j], w_s.at[0], w_r.at[0], z_peer[j]).start()
        copy(values.at[1:4], z_values.at[j], w_s.at[1], w_r.at[1], z_peer[j]).start()
        copy(own_columns.at[1:4], z_columns.at[j], w_s.at[2], w_r.at[2], z_peer[j]).start()
    for c in range(1, chunks):
        partner_copy(c).start()
    for j in range(1, GROUP):
        copy(bias, x_bias.at[j], w_s.at[3], w_r.at[3], u_peer[j]).start()

    def own_dense(layer):
        return dense(values[layer].astype(jnp.float32), own_columns[layer].astype(jnp.float32))

    w_end[0] = own_dense(0)

    def end_layer(own, other, which, layer):
        pair = jnp.concatenate([own, other], axis=1)
        preact = jnp.dot(pair, w_end[which], preferred_element_type=jnp.float32)
        return activate(preact + bias[layer : layer + 1, :])

    def first(c, _):
        partner_copy(c).wait_recv()
        for s in range(GROUP):
            act0[c, s] = end_layer(features[c, s], partner_in[c, s], 0, 0)
        for j in range(1, GROUP):
            copy(act0.at[c, z_of[j]], z_in.at[c, j], zi_s.at[c], zi_r.at[c], z_peer[j]).start()
        return 0

    lax.fori_loop(0, chunks, first, 0)

    def own_x(k, _):
        w_x[0, k] = own_dense(k + 4)
        return 0

    lax.fori_loop(0, 3, own_x, 0)
    for j in range(1, GROUP):
        copy(w_x.at[0], w_x.at[j], w_s.at[4], w_r.at[4], u_peer[j]).start()
    w_end[1] = own_dense(7)

    def many(ref, send, recv):
        return copy(ref.at[1:GROUP], ref.at[1:GROUP], send, recv, partner)

    for ref, at in ((z_bias, 0), (z_values, 1), (z_columns, 2)):
        many(ref, w_s.at[at], w_r.at[at]).wait_recv()

    def z_dense(i, _):
        j, k = i // 3, i % 3
        w_z[j, k] = dense(z_values[j, k].astype(jnp.float32), z_columns[j, k].astype(jnp.float32))
        return 0

    lax.fori_loop(0, 3 * GROUP, z_dense, 0)

    def z_layers(c, _):
        many(z_in.at[c], zi_s.at[c], zi_r.at[c]).wait_recv()
        slots = [act0[c, z]] + [z_in[c, j] for j in range(1, GROUP)]
        slots = three_layers(slots, w_z, z_bias, 1)
        back[c, 0] = slots[0]
        for j in range(1, GROUP):
            z_out[c, j] = slots[j]
        for j in range(1, GROUP):
            copy(z_out.at[c, j], back.at[c, j], zo_s.at[c], zo_r.at[c], z_peer[j]).start()
        return 0

    lax.fori_loop(0, chunks, z_layers, 0)
    many(x_bias, w_s.at[3], w_r.at[3]).wait_recv()
    many(w_x, w_s.at[4], w_r.at[4]).wait_recv()

    def to_x(c):
        many(back.at[c], zo_s.at[c], zo_r.at[c]).wait_recv()
        for j in range(1, GROUP):
            copy(back.at[c, u_of[j]], x_in.at[c, j], xi_s.at[c], xi_r.at[c], u_peer[j]).start()

    def x_layers(c):
        many(x_in.at[c], xi_s.at[c], xi_r.at[c]).wait_recv()
        slots = [back[c, u]] + [x_in[c, j] for j in range(1, GROUP)]
        slots = three_layers(slots, w_x, x_bias, 4)
        home[c, 0] = slots[0]
        for j in range(1, GROUP):
            x_out[c, j] = slots[j]
        for j in range(1, GROUP):
            copy(x_out.at[c, j], home.at[c, j], xo_s.at[c], xo_r.at[c], u_peer[j]).start()

    def last_copy(c):
        return copy(home.at[c], partner_home.at[c], pl_s.at[c], pl_r.at[c], partner)

    def to_partner(c):
        many(home.at[c], xo_s.at[c], xo_r.at[c]).wait_recv()
        last_copy(c).start()

    def last(c):
        last_copy(c).wait_recv()
        for j in range(GROUP):
            out[c, xor(zb, [(ub[k] + ((j >> k) & 1)) % 2 for k in range(3)])] = end_layer(
                home[c, j], partner_home[c, j], 1, LAYERS - 1
            )

    def steady(i, _):
        pl.when(i < chunks)(lambda: to_x(i))
        pl.when((i >= 1) & (i < chunks + 1))(lambda: x_layers(i - 1))
        pl.when((i >= 2) & (i < chunks + 2))(lambda: to_partner(i - 2))
        pl.when(i >= 3)(lambda: last(i - 3))
        return 0

    lax.fori_loop(0, chunks + 3, steady, 0)

    for ref, at in ((z_bias, 0), (z_values, 1), (z_columns, 2), (x_bias, 3), (w_x, 4)):
        many(ref, w_s.at[at], w_r.at[at]).wait_send()

    def drain(c, _):
        partner_copy(c).wait_send()
        last_copy(c).wait_send()
        many(z_in.at[c], zi_s.at[c], zi_r.at[c]).wait_send()
        many(z_out.at[c], zo_s.at[c], zo_r.at[c]).wait_send()
        many(x_in.at[c], xi_s.at[c], xi_r.at[c]).wait_send()
        many(x_out.at[c], xo_s.at[c], xo_r.at[c]).wait_send()
        return 0

    lax.fori_loop(0, chunks, drain, 0)


def shards(features, link_values, link_columns, layer_bias):
    rows, width = features.shape
    piece = rows // (CHUNKS * GROUP)
    tiled = (CHUNKS, GROUP, piece, width)
    layers, fan_in, _ = link_values.shape
    vmem = pl.BlockSpec(memory_space=pltpu.VMEM)
    act = pltpu.VMEM(tiled, jnp.bfloat16)
    links = pltpu.VMEM((GROUP, 3, fan_in, width), jnp.bfloat16)
    biases = pltpu.VMEM((GROUP, layers, width), jnp.float32)
    wide = pltpu.VMEM((GROUP, 3, 2 * width, width), jnp.bfloat16)
    out = pl.pallas_call(
        kernel,
        out_shape=jax.ShapeDtypeStruct(tiled, jnp.bfloat16),
        in_specs=[vmem] * 4,
        out_specs=vmem,
        scratch_shapes=[act] * 9
        + [
            pltpu.VMEM((layers, fan_in, width), jnp.bfloat16),
            links, links, biases, biases,
            pltpu.VMEM((2, 2 * width, width), jnp.bfloat16),
            wide, wide,
        ]
        + [pltpu.SemaphoreType.DMA((CHUNKS,))] * 12
        + [pltpu.SemaphoreType.DMA((5,))] * 2,
        compiler_params=pltpu.CompilerParams(
            collective_id=0, has_side_effects=True, vmem_limit_bytes=40 << 20
        ),
    )(features.reshape(tiled), link_values, link_columns, layer_bias)
    return out.reshape(rows, width)


def solution(mesh):
    return jax.shard_map(
        shards,
        mesh=mesh,
        in_specs=(P("row", "blk"), P(None, None, "blk"), P(None, None, "blk"), P(None, "blk")),
        out_specs=P("row", "blk"),
        check_vma=False,
    )
```

time: 297 us -> 113 us (0.38)
  the two profiles are of different devices: /device:TPU:97 before, /device:TPU:1 now
where the time goes in v1:
time: 113 us; the launch traced here: 112 us
  Pallas kernels  107 us (95%)
  local copies, waits for them, and re-layouts  4.98 us (4%)
    pallas_call x1, Pallas kernels, shards(): pl.pallas_call(kernel, out_shape=jax.ShapeDtypeStruct(tiled, jnp.bfloat16...  107 us
    unnamed x9, local copies, waits for them, and re-layouts  4.98 us

profile of v1, /device:TPU:1, one launch (start us, length us, event | category | flops | bytes accessed | tf_op | source)
XLA Modules:
  0.0 112.4 jit_solution(12461531583293197028)
XLA Ops:
  0.0 0.0 copy-start
  0.0 1.4 %copy-done = bf16[6144,128]{1,0:T(8,128)(2,1)S(1)} copy-done((bf16[6144,128]{1,0:T(8,128)(2,1)S(1)}, bf16[6144,128]{1,0:T(8,128)(2,1)}, u32[]{:S(2)}) %copy-start) | copy-done | bytes 1572888
  1.4 0.0 copy-start.1
  1.4 0.9 copy-done.1
  2.3 0.0 copy-start.2
  2.3 0.8 copy-done.2
  3.2 0.0 copy-start.3
  3.2 0.7 copy-done.3
  3.8 107.4 %shard_map.46 = bf16[8,8,96,128]{3,2,1,0:T(8,128)(2,1)S(1)} custom-call(bf16[8,8,96,128]{3,2,1,0:T(8,128)(2,1)S(1)} %bitcast.3, bf16[8,32,128]{2,1,0:T(8,128)(2,1)S(1)} %copy-done.2, s32[8,32,128]{2,1,0:T(8,128)S(1)} %copy-done.1, f32[8,128]{1,0:T(8,128)S(1)} %copy-done.3), custom_call_target="tpu_custom_call" | custom-call | tf_op jit(solution)/shard_map/pallas_call | solution.py:231
  111.2 1.1 %copy.6 = bf16[6144,128]{1,0:T(8,128)(2,1)} copy(bf16[6144,128]{1,0:T(8,128)(2,1)S(1)} %bitcast.2) | data formatting | bytes 3145728
Async XLA Ops:
  0.0 1.4 %copy-start = (bf16[6144,128]{1,0:T(8,128)(2,1)S(1)}, bf16[6144,128]{1,0:T(8,128)(2,1)}, u32[]{:S(2)}) copy-start(bf16[6144,128]{1,0:T(8,128)(2,1)} %param.4) | copy-start | bytes 4718596
  1.4 0.9 copy-start.1
  2.3 0.8 copy-start.2
  3.2 0.7 copy-start.3

commit v2 on v1

v2 whole, which is shorter than its diff:
```python
import functools

import jax
import jax.numpy as jnp
from jax import lax
from jax.experimental import pallas as pl
from jax.experimental.pallas import tpu as pltpu
from jax.sharding import PartitionSpec as P

MESH = pl.DeviceIdType.MESH
LAYERS = 8
CEILING = 4.0
CHUNKS = 16
LAGS = (7, 10, 13, 14)
GROUP = 8
MASKS = (1, 2, 4)
FAR_FIRST = (4, 5, 7, 3, 6, 2, 1)
PARTS = 4
VMEM_LIMIT = 62 << 20


def bits(value):
    return [(value // 2**k) % 2 for k in range(3)]


def xor(value_bits, mask):
    total = 0
    for k in range(3):
        flip = (mask >> k) & 1 if isinstance(mask, int) else mask[k]
        total = total + ((value_bits[k] + flip) % 2) * 2**k
    return total


def dense(links):
    width = links[0][0].shape[1]
    field = lax.broadcasted_iota(jnp.int32, (2 * width, width), 0).astype(jnp.float32)
    total = jnp.zeros((2 * width, width), jnp.float32)
    for values, columns in links:
        for link in range(values.shape[0]):
            total = total + jnp.where(field == columns[link : link + 1, :], values[link : link + 1, :], 0.0)
    return total.astype(jnp.bfloat16)


def activate(preact):
    return jnp.minimum(jnp.maximum(preact, 0.0), CEILING).astype(jnp.bfloat16)


def three_layers(slots, weights, bias):
    width = slots[0].shape[1]
    for step, mask in enumerate(MASKS):
        after = [None] * GROUP
        for low in range(GROUP):
            if low & mask:
                continue
            high = low | mask
            w_low, w_high = weights[low, step], weights[high, step]
            w_high = jnp.concatenate([w_high[width:], w_high[:width]], axis=0)
            b_pair = jnp.concatenate([bias[low, step], bias[high, step]], axis=1)
            pair = jnp.dot(
                jnp.concatenate([slots[low], slots[high]], axis=1),
                jnp.concatenate([w_low, w_high], axis=1),
                preferred_element_type=jnp.float32,
            )
            pair = activate(pair + b_pair)
            after[low], after[high] = pair[:, :width], pair[:, width:]
        slots = after
    return slots


def kernel(
    features_hbm, values_hbm, columns_hbm, bias_hbm, out_hbm,
    features, values, columns, bias, out, partner_in, act0, z_in, z_out, back, x_in, x_out, home, partner_home,
    z_links, z_bias, x_bias, w_end, w_z, w_x,
    sent, pf_r, zi_r, zo_r, xi_r, xo_r, pl_r, w_r, local,
):
    chunks, _, piece, width = features.shape
    fan_in = values.shape[1]
    loads = [
        pltpu.make_async_copy(src, dst, local.at[k])
        for k, (src, dst) in enumerate(((values_hbm, values), (columns_hbm, columns), (bias_hbm, bias)))
    ]
    for one in loads:
        one.start()
    step = chunks // PARTS
    for k in range(PARTS):
        part = pl.ds(k * step, step)
        pltpu.make_async_copy(features_hbm.at[part], features.at[part], local.at[3]).start()

    block, row = lax.axis_index("blk"), lax.axis_index("row")
    core, z, u = block % 2, (block // 2) % GROUP, block // (2 * GROUP)
    zb, ub = bits(z), bits(u)
    z_of = [xor(zb, j) for j in range(GROUP)]
    u_of = [xor(ub, j) for j in range(GROUP)]
    z_peer = [{"blk": (u * GROUP + z_of[j]) * 2 + core} for j in range(GROUP)]
    u_peer = [{"blk": (u_of[j] * GROUP + z) * 2 + core} for j in range(GROUP)]
    partner, twin = {"blk": block + 1 - 2 * core}, {"row": 1 - row}

    def copy(src, dst, send, recv, peer):
        return pltpu.make_async_remote_copy(
            src_ref=src, dst_ref=dst, send_sem=sent.at[send], recv_sem=recv, device_id=peer, device_id_type=MESH
        )

    barrier = pltpu.get_barrier_semaphore()
    peers = [partner, twin, *z_peer[1:], *u_peer[1:]]
    for peer in peers:
        pl.semaphore_signal(barrier, inc=1, device_id=peer, device_id_type=MESH)
    for one in loads:
        one.wait()
    half = fan_in // 2
    for h in range(2):
        z_links[h, 0, 0] = values[1:4, h * half : (h + 1) * half, :]
        z_links[h, 0, 1] = columns[1:4, h * half : (h + 1) * half, :].astype(jnp.float32).astype(jnp.bfloat16)
    for k in range(3):
        z_bias[0, k] = bias[k + 1 : k + 2, :]
        x_bias[0, k] = bias[k + 4 : k + 5, :]
    pltpu.make_async_copy(features_hbm, features, local.at[3]).wait()
    with jax.named_scope("barrier"):
        pl.semaphore_wait(barrier, len(peers))

    def partner_copy(c):
        return copy(features.at[c], partner_in.at[c], 0, pf_r.at[c], partner)

    partner_copy(0).start()
    for j in FAR_FIRST:
        copy(z_links.at[row, 0], z_links.at[row, j], 6, w_r.at[0], z_peer[j]).start()
        copy(z_bias.at[0], z_bias.at[j], 7, w_r.at[1], z_peer[j]).start()
    for c in range(1, chunks):
        partner_copy(c).start()

    def own_dense(layer):
        return dense([(values[layer].astype(jnp.float32), columns[layer].astype(jnp.float32))])

    with jax.named_scope("w0"):
        w_end[0] = own_dense(0)

    def end_layer(own, other, which, layer):
        pair = jnp.concatenate([own, other], axis=1)
        preact = jnp.dot(pair, w_end[which], preferred_element_type=jnp.float32)
        return preact + bias[layer : layer + 1, :]

    def first(c, _):
        with jax.named_scope("pf_wait"):
            partner_copy(c).wait_recv()
        for s in range(GROUP):
            act0[c, s] = activate(end_layer(features[c, s], partner_in[c, s], 0, 0))
        for j in FAR_FIRST:
            copy(act0.at[c, z_of[j]], z_in.at[c, j], 1, zi_r.at[c], z_peer[j]).start()
        return 0

    lax.fori_loop(0, chunks, first, 0)

    def own_x(k, _):
        w_x[0, k] = own_dense(k + 4)
        return 0

    with jax.named_scope("own_x"):
        lax.fori_loop(0, 3, own_x, 0)
    w_end[1] = own_dense(7)

    def many(ref, send, recv):
        return copy(ref.at[1:GROUP], ref.at[1:GROUP], send, recv, partner)

    def links_from(r, peer, send, recv):
        return copy(z_links.at[r, 1:GROUP], z_links.at[r, 1:GROUP], send, recv, peer)

    with jax.named_scope("zw_wait"):
        links_from(row, twin, 6, w_r.at[0]).wait_recv()
    links_from(row, twin, 8, w_r.at[2]).start()
    for j in range(1, GROUP):
        copy(x_bias.at[0], x_bias.at[j], 9, w_r.at[3], u_peer[j]).start()
        copy(w_x.at[0], w_x.at[j], 10, w_r.at[4], u_peer[j]).start()
    with jax.named_scope("tw_wait"):
        many(z_bias, 7, w_r.at[1]).wait_recv()
        links_from(1 - row, twin, 8, w_r.at[2]).wait_recv()

    def z_dense(i, _):
        j, k = i // 3, i % 3
        w_z[j, k] = dense(
            [(z_links[h, j, 0, k].astype(jnp.float32), z_links[h, j, 1, k].astype(jnp.float32)) for h in range(2)]
        )
        return 0

    with jax.named_scope("z_dense"):
        lax.fori_loop(0, 3 * GROUP, z_dense, 0)

    def z_layers(c):
        with jax.named_scope("zin_wait"):
            many(z_in.at[c], 1, zi_r.at[c]).wait_recv()
        slots = [act0[c, z]] + [z_in[c, j] for j in range(1, GROUP)]
        slots = three_layers(slots, w_z, z_bias)
        back[c, 0] = slots[0]
        for j in range(1, GROUP):
            z_out[c, j] = slots[j]
        for j in FAR_FIRST:
            copy(z_out.at[c, j], back.at[c, j], 2, zo_r.at[c], z_peer[j]).start()

    def to_x(c):
        with jax.named_scope("zout_wait"):
            many(back.at[c], 2, zo_r.at[c]).wait_recv()
        for j in range(1, GROUP):
            copy(back.at[c, u_of[j]], x_in.at[c, j], 3, xi_r.at[c], u_peer[j]).start()

    def x_weights():
        with jax.named_scope("xw_wait"):
            many(x_bias, 9, w_r.at[3]).wait_recv()
            many(w_x, 10, w_r.at[4]).wait_recv()

    def x_layers(c):
        pl.when(c == 0)(x_weights)
        with jax.named_scope("xin_wait"):
            many(x_in.at[c], 3, xi_r.at[c]).wait_recv()
        slots = [back[c, u]] + [x_in[c, j] for j in range(1, GROUP)]
        slots = three_layers(slots, w_x, x_bias)
        home[c, 0] = slots[0]
        for j in range(1, GROUP):
            x_out[c, j] = slots[j]
        for j in range(1, GROUP):
            copy(x_out.at[c, j], home.at[c, j], 4, xo_r.at[c], u_peer[j]).start()

    def last_copy(c):
        return copy(home.at[c], partner_home.at[c], 5, pl_r.at[c], partner)

    def to_partner(c):
        with jax.named_scope("xout_wait"):
            many(home.at[c], 4, xo_r.at[c]).wait_recv()
        last_copy(c).start()

    def last(c):
        with jax.named_scope("pl_wait"):
            last_copy(c).wait_recv()
        for j in range(GROUP):
            preact = end_layer(home[c, j], partner_home[c, j], 1, LAYERS - 1)
            at = xor(zb, [(ub[k] + ((j >> k) & 1)) % 2 for k in range(3)])
            out[c, at] = jnp.minimum(preact, CEILING).astype(jnp.bfloat16)
        pltpu.make_async_copy(out.at[c], out_hbm.at[c], local.at[4]).start()

    def steady(i, _):
        pl.when(i < chunks)(lambda: z_layers(i))
        for stage, lag in zip((to_x, x_layers, to_partner, last), LAGS):
            pl.when((i >= lag) & (i < chunks + lag))(functools.partial(stage, i - lag))
        return 0

    lax.fori_loop(0, chunks + LAGS[-1], steady, 0)

    with jax.named_scope("drain"):
        for at, ref in (
            (0, features),
            (1, z_in.at[:, 1:GROUP]),
            (2, z_out.at[:, 1:GROUP]),
            (3, x_in.at[:, 1:GROUP]),
            (4, x_out.at[:, 1:GROUP]),
            (5, home),
            (6, z_links.at[0, 1:GROUP]),
            (7, z_bias.at[1:GROUP]),
            (8, z_links.at[0, 1:GROUP]),
            (9, x_bias.at[1:GROUP]),
            (10, w_x.at[1:GROUP]),
        ):
            copy(ref, ref, at, w_r.at[0], partner).wait_send()
        pltpu.make_async_copy(out, out_hbm, local.at[4]).wait()


def finish_kernel(source, result, before, after, arrived, stored):
    loads = [pltpu.make_async_copy(source.at[k], before.at[k], arrived.at[k]) for k in range(PARTS)]
    stores = [pltpu.make_async_copy(after.at[k], result.at[k], stored.at[k]) for k in range(PARTS)]
    for one in loads:
        one.start()
    for k in range(PARTS):
        loads[k].wait()
        after[k] = jnp.maximum(before[k], 0)
        stores[k].start()
    for one in stores:
        one.wait()


def shards(features, link_values, link_columns, layer_bias):
    rows, width = features.shape
    piece = rows // (CHUNKS * GROUP)
    tiled = (CHUNKS, GROUP, piece, width)
    layers, fan_in, _ = link_values.shape
    hbm = pl.BlockSpec(memory_space=pltpu.HBM)
    act = pltpu.VMEM(tiled, jnp.bfloat16)
    biases = pltpu.VMEM((GROUP, 3, 1, width), jnp.float32)
    wide = pltpu.VMEM((GROUP, 3, 2 * width, width), jnp.bfloat16)
    out = pl.pallas_call(
        kernel,
        out_shape=jax.ShapeDtypeStruct(tiled, jnp.bfloat16),
        in_specs=[hbm] * 4,
        out_specs=hbm,
        scratch_shapes=[
            act,
            pltpu.VMEM(link_values.shape, jnp.bfloat16),
            pltpu.VMEM(link_columns.shape, jnp.int32),
            pltpu.VMEM(layer_bias.shape, jnp.float32),
        ]
        + [act] * 10
        + [
            pltpu.VMEM((2, GROUP, 2, 3, fan_in // 2, width), jnp.bfloat16),
            biases,
            biases,
            pltpu.VMEM((2, 2 * width, width), jnp.bfloat16),
            wide,
            wide,
            pltpu.SemaphoreType.DMA((11,)),
        ]
        + [pltpu.SemaphoreType.DMA((CHUNKS,))] * 6
        + [pltpu.SemaphoreType.DMA((5,))] * 2,
        compiler_params=pltpu.CompilerParams(
            collective_id=0, has_side_effects=True, vmem_limit_bytes=VMEM_LIMIT
        ),
    )(features.reshape(tiled), link_values, link_columns, layer_bias)
    parts = (PARTS, rows // PARTS, width)
    result = pl.pallas_call(
        finish_kernel,
        out_shape=jax.ShapeDtypeStruct(parts, jnp.bfloat16),
        in_specs=[hbm],
        out_specs=hbm,
        scratch_shapes=[pltpu.VMEM(parts, jnp.bfloat16)] * 2 + [pltpu.SemaphoreType.DMA((PARTS,))] * 2,
        compiler_params=pltpu.CompilerParams(vmem_limit_bytes=VMEM_LIMIT),
    )(out.reshape(parts))
    return result.reshape(rows, width)


def solution(mesh):
    return jax.shard_map(
        shards,
        mesh=mesh,
        in_specs=(P("row", "blk"), P(None, None, "blk"), P(None, None, "blk"), P(None, "blk")),
        out_specs=P("row", "blk"),
        check_vma=False,
    )
```

time: 113 us -> 103 us (0.912)
  Pallas kernels: 107 us -> 102 us
  local copies, waits for them, and re-layouts: 4.98 us -> 0 us
    pallas_call x1, Pallas kernels: 107 us -> 100 us  [shards(): pl.pallas_call(kernel, out_shape=jax.ShapeDtypeStruct(tiled, jnp.bfloat16...]
    unnamed x9 -> x0, local copies, waits for them, and re-layouts: 4.98 us -> none
    pallas_call x0 -> x1, Pallas kernels: none -> 2.26 us  [shards(): pl.pallas_call(finish_kernel, out_shape=jax.ShapeDtypeStruct(parts, jnp.b...]
where the time goes in v2:
time: 103 us; the launch traced here: 102 us
  Pallas kernels  102 us (99%)
    pallas_call x1, Pallas kernels, shards(): pl.pallas_call(kernel, out_shape=jax.ShapeDtypeStruct(tiled, jnp.bfloat16...  100 us
    pallas_call x1, Pallas kernels, shards(): pl.pallas_call(finish_kernel, out_shape=jax.ShapeDtypeStruct(parts, jnp.b...  2.26 us

profile of v2, /device:TPU:1, one launch (start us, length us, event | category | flops | bytes accessed | tf_op | source)
XLA Modules:
  0.0 102.4 jit_solution(4679255386161530313)
XLA Ops:
  0.0 100.1 %shard_map.46 = bf16[16,8,48,128]{3,2,1,0:T(8,128)(2,1)} custom-call(bf16[16,8,48,128]{3,2,1,0:T(8,128)(2,1)} %bitcast.4, bf16[8,32,128]{2,1,0:T(8,128)(2,1)} %values_hbm.1, s32[8,32,128]{2,1,0:T(8,128)} %columns_hbm.1, f32[8,128]{1,0:T(8,128)} %bias_hbm.1), custom_call_target="tpu_custom_call" | custom-call | tf_op jit(solution)/shard_map/pallas_call | solution.py:285
  100.1 2.3 %shard_map.47 = bf16[4,1536,128]{2,1,0:T(8,128)(2,1)} custom-call(bf16[4,1536,128]{2,1,0:T(8,128)(2,1)} %bitcast.3), custom_call_target="tpu_custom_call" | custom-call | tf_op jit(solution)/shard_map/pallas_call | solution.py:313

commit v3 on v2

--- a/solution.py
+++ b/solution.py
@@ -11,10 +11,12 @@
 LAYERS = 8
 CEILING = 4.0
 CHUNKS = 16
-LAGS = (7, 10, 13, 14)
+LAGS = (7, 10, 13, 16)
 GROUP = 8
 MASKS = (1, 2, 4)
 FAR_FIRST = (4, 5, 7, 3, 6, 2, 1)
+X_FAR_FIRST = (5, 3, 7, 1, 4, 2, 6)
+BOTH = 1
 PARTS = 4
 VMEM_LIMIT = 62 << 20
 
@@ -31,14 +33,14 @@
     return total
 
 
-def dense(links):
-    width = links[0][0].shape[1]
+def dense(values, columns):
+    width = values.shape[1]
+    values, columns = values.astype(jnp.float32), columns.astype(jnp.float32)
     field = lax.broadcasted_iota(jnp.int32, (2 * width, width), 0).astype(jnp.float32)
     total = jnp.zeros((2 * width, width), jnp.float32)
-    for values, columns in links:
-        for link in range(values.shape[0]):
-            total = total + jnp.where(field == columns[link : link + 1, :], values[link : link + 1, :], 0.0)
-    return total.astype(jnp.bfloat16)
+    for link in range(values.shape[0]):
+        total = total + jnp.where(field == columns[link : link + 1, :], values[link : link + 1, :], 0.0)
+    return total
 
 
 def activate(preact):
@@ -70,7 +72,7 @@
 def kernel(
     features_hbm, values_hbm, columns_hbm, bias_hbm, out_hbm,
     features, values, columns, bias, out, partner_in, act0, z_in, z_out, back, x_in, x_out, home, partner_home,
-    z_links, z_bias, x_bias, w_end, w_z, w_x,
+    partial, z_links, z_bias, x_bias, w_end, w_z, w_x,
     sent, pf_r, zi_r, zo_r, xi_r, xo_r, pl_r, w_r, local,
 ):
     chunks, _, piece, width = features.shape
@@ -93,6 +95,7 @@
     u_of = [xor(ub, j) for j in range(GROUP)]
     z_peer = [{"blk": (u * GROUP + z_of[j]) * 2 + core} for j in range(GROUP)]
     u_peer = [{"blk": (u_of[j] * GROUP + z) * 2 + core} for j in range(GROUP)]
+    other = [{"blk": (u_of[j] * GROUP + z) * 2 + 1 - core} for j in range(GROUP)]
     partner, twin = {"blk": block + 1 - 2 * core}, {"row": 1 - row}
 
     def copy(src, dst, send, recv, peer):
@@ -101,7 +104,7 @@
         )
 
     barrier = pltpu.get_barrier_semaphore()
-    peers = [partner, twin, *z_peer[1:], *u_peer[1:]]
+    peers = [partner, twin, *z_peer[1:], *u_peer[1:], *other[1:]]
     for peer in peers:
         pl.semaphore_signal(barrier, inc=1, device_id=peer, device_id_type=MESH)
     for one in loads:
@@ -128,7 +131,7 @@
         partner_copy(c).start()
 
     def own_dense(layer):
-        return dense([(values[layer].astype(jnp.float32), columns[layer].astype(jnp.float32))])
+        return dense(values[layer], columns[layer]).astype(jnp.bfloat16)
 
     with jax.named_scope("w0"):
         w_end[0] = own_dense(0)
@@ -163,25 +166,41 @@
     def links_from(r, peer, send, recv):
         return copy(z_links.at[r, 1:GROUP], z_links.at[r, 1:GROUP], send, recv, peer)
 
+    def loop(first_step, last_step, body):
+        lax.fori_loop(first_step, last_step, lambda i, _: (body(i), 0)[1], 0)
+
+    def send_w_x(j):
+        copy(x_bias.at[0], x_bias.at[j], 9, w_r.at[3], u_peer[j]).start()
+        copy(w_x.at[0], w_x.at[j], 10, w_r.at[4], u_peer[j]).start()
+
+    for j in (2, 4, 6):
+        send_w_x(j)
+
+    def z_own(k):
+        w_z[0, k] = own_dense(k + 1)
+
+    def z_half(h, i):
+        return dense(z_links[h, i // 3, 0, i % 3], z_links[h, i // 3, 1, i % 3])
+
+    def z_first(i):
+        partial[i // 3, i % 3] = z_half(row, i)
+
+    def z_second(i):
+        w_z[i // 3, i % 3] = (partial[i // 3, i % 3] + z_half(1 - row, i)).astype(jnp.bfloat16)
+
+    loop(0, 3, z_own)
     with jax.named_scope("zw_wait"):
         links_from(row, twin, 6, w_r.at[0]).wait_recv()
     links_from(row, twin, 8, w_r.at[2]).start()
-    for j in range(1, GROUP):
-        copy(x_bias.at[0], x_bias.at[j], 9, w_r.at[3], u_peer[j]).start()
-        copy(w_x.at[0], w_x.at[j], 10, w_r.at[4], u_peer[j]).start()
+    for j in (1, 5, 3, 7):
+        send_w_x(j)
+    with jax.named_scope("z_first"):
+        loop(3, 3 * GROUP, z_first)
     with jax.named_scope("tw_wait"):
         many(z_bias, 7, w_r.at[1]).wait_recv()
         links_from(1 - row, twin, 8, w_r.at[2]).wait_recv()
-
-    def z_dense(i, _):
-        j, k = i // 3, i % 3
-        w_z[j, k] = dense(
-            [(z_links[h, j, 0, k].astype(jnp.float32), z_links[h, j, 1, k].astype(jnp.float32)) for h in range(2)]
-        )
-        return 0
-
     with jax.named_scope("z_dense"):
-        lax.fori_loop(0, 3 * GROUP, z_dense, 0)
+        loop(3, 3 * GROUP, z_second)
 
     def z_layers(c):
         with jax.named_scope("zin_wait"):
@@ -197,7 +216,7 @@
     def to_x(c):
         with jax.named_scope("zout_wait"):
             many(back.at[c], 2, zo_r.at[c]).wait_recv()
-        for j in range(1, GROUP):
+        for j in X_FAR_FIRST:
             copy(back.at[c, u_of[j]], x_in.at[c, j], 3, xi_r.at[c], u_peer[j]).start()
 
     def x_weights():
@@ -214,8 +233,19 @@
         home[c, 0] = slots[0]
         for j in range(1, GROUP):
             x_out[c, j] = slots[j]
-        for j in range(1, GROUP):
-            copy(x_out.at[c, j], home.at[c, j], 4, xo_r.at[c], u_peer[j]).start()
+
+        def to_both():
+            for j in X_FAR_FIRST:
+                copy(x_out.at[c, j], home.at[c, j], 4, xo_r.at[c], u_peer[j]).start()
+                copy(x_out.at[c, j], partner_home.at[c, j], 5, pl_r.at[c], other[j]).start()
+            copy(home.at[c, 0], partner_home.at[c, 0], 5, pl_r.at[c], partner).start()
+
+        def to_one():
+            for j in X_FAR_FIRST:
+                copy(x_out.at[c, j], home.at[c, j], 4, xo_r.at[c], u_peer[j]).start()
+
+        pl.when(c >= chunks - BOTH)(to_both)
+        pl.when(c < chunks - BOTH)(to_one)
 
     def last_copy(c):
         return copy(home.at[c], partner_home.at[c], 5, pl_r.at[c], partner)
@@ -223,7 +253,7 @@
     def to_partner(c):
         with jax.named_scope("xout_wait"):
             many(home.at[c], 4, xo_r.at[c]).wait_recv()
-        last_copy(c).start()
+        pl.when(c < chunks - BOTH)(lambda: last_copy(c).start())
 
     def last(c):
         with jax.named_scope("pl_wait"):
@@ -295,6 +325,7 @@
         ]
         + [act] * 10
         + [
+            pltpu.VMEM((GROUP, 3, 2 * width, width), jnp.float32),
             pltpu.VMEM((2, GROUP, 2, 3, fan_in // 2, width), jnp.bfloat16),
             biases,
             biases,

time: 103 us -> 101 us (0.981)
    pallas_call x1, Pallas kernels: 100 us -> 98.7 us  [shards(): pl.pallas_call(kernel, out_shape=jax.ShapeDtypeStruct(tiled, jnp.bfloat16...]
where the time goes in v3:
time: 101 us
  Pallas kernels  101 us (100%)
    pallas_call x1, Pallas kernels, shards(): pl.pallas_call(kernel, out_shape=jax.ShapeDtypeStruct(tiled, jnp.bfloat16...  98.7 us
    pallas_call x1, Pallas kernels, shards(): pl.pallas_call(finish_kernel, out_shape=jax.ShapeDtypeStruct(parts, jnp.b...  2.26 us

profile of v3, /device:TPU:1, one launch (start us, length us, event | category | flops | bytes accessed | tf_op | source)
XLA Modules:
  0.0 100.9 jit_solution(1680924596578173478)
XLA Ops:
  0.0 98.7 %shard_map.46 = bf16[16,8,48,128]{3,2,1,0:T(8,128)(2,1)} custom-call(bf16[16,8,48,128]{3,2,1,0:T(8,128)(2,1)} %bitcast.4, bf16[8,32,128]{2,1,0:T(8,128)(2,1)} %values_hbm.1, s32[8,32,128]{2,1,0:T(8,128)} %columns_hbm.1, f32[8,128]{1,0:T(8,128)} %bias_hbm.1), custom_call_target="tpu_custom_call" | custom-call | tf_op jit(solution)/shard_map/pallas_call | solution.py:315
  98.7 2.3 %shard_map.47 = bf16[4,1536,128]{2,1,0:T(8,128)(2,1)} custom-call(bf16[4,1536,128]{2,1,0:T(8,128)(2,1)} %bitcast.3), custom_call_target="tpu_custom_call" | custom-call | tf_op jit(solution)/shard_map/pallas_call | solution.py:344

commit v4 on v3

--- a/solution.py
+++ b/solution.py
@@ -10,12 +10,12 @@
 MESH = pl.DeviceIdType.MESH
 LAYERS = 8
 CEILING = 4.0
-CHUNKS = 16
-LAGS = (7, 10, 13, 16)
+CHUNKS = 12
+LAGS = (5, 7, 9, 11)
 GROUP = 8
 MASKS = (1, 2, 4)
 FAR_FIRST = (4, 5, 7, 3, 6, 2, 1)
-X_FAR_FIRST = (5, 3, 7, 1, 4, 2, 6)
+X_FAR_FIRST = (5, 7, 3, 4, 1, 6, 2)
 BOTH = 1
 PARTS = 4
 VMEM_LIMIT = 62 << 20

time: 101 us -> 101 us (level)
  no operation moved by 1% of the time
where the time goes in v4:
time: 101 us; the launch traced here: 100 us
  Pallas kernels  100 us (99%)
    pallas_call x1, Pallas kernels, shards(): pl.pallas_call(kernel, out_shape=jax.ShapeDtypeStruct(tiled, jnp.bfloat16...  98.2 us
    pallas_call x1, Pallas kernels, shards(): pl.pallas_call(finish_kernel, out_shape=jax.ShapeDtypeStruct(parts, jnp.b...  2.26 us

profile of v4, /device:TPU:1, one launch (start us, length us, event | category | flops | bytes accessed | tf_op | source)
XLA Modules:
  0.0 100.5 jit_solution(66955674737984203)
XLA Ops:
  0.0 98.2 %shard_map.46 = bf16[12,8,64,128]{3,2,1,0:T(8,128)(2,1)} custom-call(bf16[12,8,64,128]{3,2,1,0:T(8,128)(2,1)} %bitcast.4, bf16[8,32,128]{2,1,0:T(8,128)(2,1)} %values_hbm.1, s32[8,32,128]{2,1,0:T(8,128)} %columns_hbm.1, f32[8,128]{1,0:T(8,128)} %bias_hbm.1), custom_call_target="tpu_custom_call" | custom-call | tf_op jit(solution)/shard_map/pallas_call | solution.py:315
  98.2 2.3 %shard_map.47 = bf16[4,1536,128]{2,1,0:T(8,128)(2,1)} custom-call(bf16[4,1536,128]{2,1,0:T(8,128)(2,1)} %bitcast.3), custom_call_target="tpu_custom_call" | custom-call | tf_op jit(solution)/shard_map/pallas_call | solution.py:344

commit v5 on v4

--- a/solution.py
+++ b/solution.py
@@ -16,7 +16,7 @@
 MASKS = (1, 2, 4)
 FAR_FIRST = (4, 5, 7, 3, 6, 2, 1)
 X_FAR_FIRST = (5, 7, 3, 4, 1, 6, 2)
-BOTH = 1
+BOTH = 2
 PARTS = 4
 VMEM_LIMIT = 62 << 20
 

time: 101 us -> 101 us (level)
  no operation moved by 1% of the time
where the time goes in v5:
time: 101 us
  Pallas kernels  101 us (100%)
    pallas_call x1, Pallas kernels, shards(): pl.pallas_call(kernel, out_shape=jax.ShapeDtypeStruct(tiled, jnp.bfloat16...  98.4 us
    pallas_call x1, Pallas kernels, shards(): pl.pallas_call(finish_kernel, out_shape=jax.ShapeDtypeStruct(parts, jnp.b...  2.26 us

profile of v5, /device:TPU:1, one launch (start us, length us, event | category | flops | bytes accessed | tf_op | source)
XLA Modules:
  0.0 100.6 jit_solution(981815254945709499)
XLA Ops:
  0.0 98.4 %shard_map.46 = bf16[12,8,64,128]{3,2,1,0:T(8,128)(2,1)} custom-call(bf16[12,8,64,128]{3,2,1,0:T(8,128)(2,1)} %bitcast.4, bf16[8,32,128]{2,1,0:T(8,128)(2,1)} %values_hbm.1, s32[8,32,128]{2,1,0:T(8,128)} %columns_hbm.1, f32[8,128]{1,0:T(8,128)} %bias_hbm.1), custom_call_target="tpu_custom_call" | custom-call | tf_op jit(solution)/shard_map/pallas_call | solution.py:315
  98.4 2.3 %shard_map.47 = bf16[4,1536,128]{2,1,0:T(8,128)(2,1)} custom-call(bf16[4,1536,128]{2,1,0:T(8,128)(2,1)} %bitcast.3), custom_call_target="tpu_custom_call" | custom-call | tf_op jit(solution)/shard_map/pallas_call | solution.py:344
